TPU v7x, 32 devices: a whole 2x2x4 slice. The times are simulated.
32 devices in a mesh: groups: 2 (over x), rows: 16 (over z, y, core).
Axes of the slice: x: 2, y: 2, z: 4, core: 2. Of those that a mesh axis runs over, the one named last changes fastest.
Arguments:
- frames: bfloat16 [16384, 2560], P(('groups', 'rows')), parts along dimension 0, may hold values from -6 to 6
- offsets: int32 [4096], P(('groups', 'rows')), parts along dimension 0, may hold values from 0 to 8173, as said below
- neighbours: int32 [32, 4096], P(None, ('groups', 'rows')), parts along dimension 1, may hold values from 0 to 2047, as said below
- initial_codes: int32 [32, 4096], P(None, ('groups', 'rows')), parts along dimension 1, may hold values from -1048576 to 1048575
- embed_weight: bfloat16 [2560, 256], replicated, may hold values from -0.125 to 0.125
- embed_bias: float32 [256], replicated, may hold values from -0.9 to 0.9
Outputs:
- affinity: float32 [32, 4096], P(None, ('groups', 'rows')), parts along dimension 1
- vectors: float32 [32, 4096], P(None, ('groups', 'rows')), parts along dimension 1
There are 2 independent parts, one for each index of `groups`. A program takes and returns all parts, laid end to end along the dimension named above; an argument that names none is the same for every part. Nothing has to cross between parts.
Inputs may be any that keep to these rules, and one draw needn't show every extreme that they name: `offsets`: the window of row i starts in the block of 512 frames numbered i // 128 and its 19 frames end before frame 8192. `neighbours`: the 32 columns of row i are distinct and differ from i; the k-th is (i + d) mod 2048 with 1 + k s <= d <= (k + 1) s, where s = 63.
All inputs are finite; a program needn't handle non-finite values.
Results may differ from a plain program's by a relative error of at most 0.012.
The roundings to bfloat16 on the way count: a program that leaves them out, or rounds other values in their place, can miss the bound.
Values may be sent and summed in bfloat16 or wider, within the bound.
No kernel may reach another device: no remote copies, remote signals or barrier semaphores. Data moves between devices by JAX's collectives and lax.ppermute only.
A program may use at most 64 MiB of HBM per device.

v0:
```python
import jax
import jax.numpy as jnp
from jax import lax
from jax.sharding import PartitionSpec as P

WIN = 19
ITERS = 3
epsilon = 1e-06
sharpness = 8.0
seed_scale = 2.0 ** (-20)


def from_behind(block, axis, distance):
    devices = range(lax.axis_size(axis))
    route = [(i - distance, i) for i in devices if i - distance in devices]
    return lax.ppermute(block, axis, route)


def block_width(length, shard_rows):
    shards = length // shard_rows
    chosen = 1
    for factor in range(1, shards + 1):
        if shards % factor == 0 and factor * shard_rows <= 4096:
            chosen = factor
    return chosen * shard_rows


def on_device(frames, offsets, neighbours, initial_codes, embed_weight, embed_bias):
    own_rows = offsets.shape[0]
    own_frames = frames.shape[0]
    kept = neighbours.shape[0]
    my_index = lax.axis_index("rows")
    next_frames = from_behind(frames[: WIN - 1], "rows", -1)
    extended = jnp.concatenate([frames, next_frames], axis=0)
    window_start = offsets - my_index * own_frames
    positions = jnp.arange(extended.shape[0], dtype=jnp.int32)[None, :]
    begins = window_start[:, None]
    window_mask = ((positions >= begins) & (positions < begins + WIN)).astype(jnp.bfloat16)
    window_sums = jnp.dot(window_mask, extended, preferred_element_type=jnp.float32)
    pooled = (window_sums * (1.0 / WIN)).astype(jnp.bfloat16)
    embedded = jnp.dot(pooled, embed_weight, preferred_element_type=jnp.float32) + embed_bias
    squares = jnp.sum(embedded * embedded, axis=1, keepdims=True)
    unit_rows = (embedded * lax.rsqrt(squares + epsilon)).astype(jnp.bfloat16)
    portion = lax.all_gather(unit_rows, "rows", axis=0, tiled=True)
    length = portion.shape[0]
    block_cols = block_width(length, own_rows)

    def one_block(block_index, carried):
        first_col = block_index * block_cols
        candidates = lax.dynamic_slice_in_dim(portion, first_col, block_cols, 0)
        scores = lax.dot_general(
            unit_rows, candidates, (((1,), (1,)), ((), ())), preferred_element_type=jnp.float32
        )
        relative = neighbours - first_col
        inside = (relative >= 0) & (relative < block_cols)
        picked = jnp.take_along_axis(scores, jnp.clip(relative, 0, block_cols - 1).T, axis=1).T
        return carried + jnp.where(inside, picked, 0.0)

    cosine = lax.fori_loop(
        0, length // block_cols, one_block, jnp.zeros((kept, own_rows), jnp.float32)
    )
    affinity = jnp.exp(sharpness * (cosine - 1.0))
    vectors = initial_codes.astype(jnp.float32) * seed_scale
    vec_count = vectors.shape[0]
    carried = vectors
    for turn_index in range(ITERS):
        gathered = lax.all_gather(carried, "rows", axis=1, tiled=True)
        if turn_index > 0:
            gram_matrix = jnp.dot(gathered, gathered.T, precision=lax.Precision.HIGHEST)
            cholesky_factor = jnp.linalg.cholesky(gram_matrix)
            gathered = jax.scipy.linalg.solve_triangular(cholesky_factor, gathered, lower=True)
        current = lax.dynamic_slice_in_dim(gathered, my_index * own_rows, own_rows, 1)
        forward = jnp.sum(affinity[None] * jnp.take(gathered, neighbours, axis=1), axis=1)
        spread = (
            jnp.zeros((vec_count, gathered.shape[1]), jnp.float32)
            .at[:, neighbours.reshape(-1)]
            .add((affinity[None] * current[:, None, :]).reshape(vec_count, -1))
        )
        mixed = 0.5 * (forward + lax.psum_scatter(spread, "rows", scatter_dimension=1, tiled=True))
        carried = mixed
    partial_gram = jnp.dot(carried, carried.T, precision=lax.Precision.HIGHEST)
    gram_matrix = lax.psum(partial_gram, "rows")
    cholesky_factor = jnp.linalg.cholesky(gram_matrix)
    carried = jax.scipy.linalg.solve_triangular(cholesky_factor, carried, lower=True)
    return (affinity, carried)


def solution(mesh):
    placed = (
        P(("groups", "rows"), None),
        P(("groups", "rows")),
        P(None, ("groups", "rows")),
        P(None, ("groups", "rows")),
        P(),
        P(),
    )
    return jax.shard_map(
        on_device,
        mesh=mesh,
        in_specs=placed,
        out_specs=(P(None, ("groups", "rows")), P(None, ("groups", "rows"))),
        check_vma=False,
    )
```

profile of v0, /device:TPU:0, one launch (start us, length us, event | category | flops | bytes accessed | tf_op | source)
XLA Modules:
  0.0 474.0 jit_solution(6266484893465082726)
XLA Ops:
  7.2 1.0 slice.17
  8.2 1.3 collective-permute-start
  9.5 0.7 broadcast_add_fusion
  10.2 1.3 collective-permute-done
  11.5 2.9 multiply_reduce_fusion
  14.3 0.7 multiply_convert_fusion
  15.4 25.2 %all_gather.13 = f32[32,2048]{1,0:T(8,128)S(1)} all-gather(f32[32,128]{1,0:T(8,128)S(1)} %convert_multiply_fusion), channel_id=1, replica_groups=mesh['groups'=2,'rows'=16] {'rows'}, dimensions={1}, use_global_device_ids=true | all-gather | bytes 278528 | tf_op jit(solution)/shard_map/all_gather | solution.py:67
  41.1 14.1 %gather_fusion.1 = f32[4096,32]{1,0:T(8,128)} fusion(f32[32,2048]{0,1:T(8,128)S(1)} %copy.50, s32[4096]{0:T(1024)S(1)} %bitcast_clamp_fusion), kind=kCustom, calls=%fused_computation.clone | custom fusion | bytes 1064960 | tf_op jit(solution)/shard_map/jit(_take)/gather | solution.py:73
  55.2 3.1 all-gather.2.cloned.1.call-done
  58.3 1.7 fusion.64
  60.0 32.8 %gather_fusion = f32[4096]{0:T(1024)S(1)} fusion(f32[128,2048]{1,0:T(8,128)S(1)} %fusion.64, s32[4096]{0:T(1024)S(1)} %reshape.113), kind=kCustom, calls=%fused_computation.3 | custom fusion | bytes 65536 | tf_op jit(solution)/shard_map/while/body/eval_jaxpr/jit(take_along_axis)/gather | solution.py:56
  93.6 23.4 %scatter_custom_fusion = f32[32,2048]{0,1:T(8,128)} fusion(s32[4096]{0:T(1024)S(1)} %bitcast.98, f32[32,4096]{0,1:T(8,128)S(1)} %bitcast_multiply_fusion.4, f32[]{:T(128)} %constant.102.clone.1), kind=kCustom, calls=%fused_computation.22 | custom fusion | flops 131072 | bytes 2359300 | tf_op jit(solution)/shard_map/scatter-add | solution.py:77
  117.1 3.2 fusion.12
  120.3 53.4 %reduce-scatter.4.cloned.1.call-done = f32[32,128]{0,1:T(8,128)} async-done(((f32[32,2048]{0,1:T(8,128)}), f32[32,128]{0,1:T(8,128)}) %reduce-scatter.4.cloned.1.call-update) | async-done | bytes 16400 | tf_op jit(solution)/shard_map/reduce_scatter | solution.py:79
  173.7 0.8 add_multiply_fusion.2
  174.6 22.6 %all_gather.14 = f32[32,2048]{0,1:T(8,128)S(1)} all-gather(f32[32,128]{0,1:T(8,128)S(1)} %add_multiply_fusion.2), channel_id=1, replica_groups=mesh['groups'=2,'rows'=16] {'rows'}, dimensions={1}, use_global_device_ids=true | all-gather | bytes 278528 | tf_op jit(solution)/shard_map/all_gather | solution.py:67
  197.1 1.8 fusion.65
  199.0 2.9 cholesky.59
  202.0 0.6 compare_reduce_fusion.2
  202.6 0.7 fusion.40
  203.3 2.4 custom-call.13
  205.7 1.2 fusion.48
  207.0 0.7 copy-done.2
  208.4 23.4 %scatter_custom_fusion.1 = f32[32,2048]{0,1:T(8,128)} fusion(s32[4096]{0:T(1024)S(1)} %bitcast.99, f32[32,4096]{0,1:T(8,128)S(1)} %bitcast_multiply_fusion.2, f32[]{:T(128)} %constant.102.clone.1), kind=kCustom, calls=%fused_computation.17 | custom fusion | flops 131072 | bytes 2359300 | tf_op jit(solution)/shard_map/scatter-add | solution.py:77
  232.0 1.3 copy.54
  233.3 14.1 %gather_fusion.2 = f32[4096,32]{1,0:T(8,128)} fusion(f32[32,2048]{0,1:T(8,128)S(1)} %copy.54, s32[4096]{0:T(1024)S(1)} %bitcast_clamp_fusion), kind=kCustom, calls=%fused_computation.1.clone | custom fusion | bytes 1064960 | tf_op jit(solution)/shard_map/jit(_take)/gather | solution.py:73
  247.4 3.2 fusion.9
  250.6 36.3 %reduce-scatter.6.cloned.1.call-done = f32[32,128]{0,1:T(8,128)} async-done(((f32[32,2048]{0,1:T(8,128)}), f32[32,128]{0,1:T(8,128)}) %reduce-scatter.6.cloned.1.call-update) | async-done | bytes 16400 | tf_op jit(solution)/shard_map/reduce_scatter | solution.py:79
  286.9 0.8 add_multiply_fusion.1
  287.8 22.6 %all_gather.15 = f32[32,2048]{0,1:T(8,128)S(1)} all-gather(f32[32,128]{0,1:T(8,128)S(1)} %add_multiply_fusion.1), channel_id=1, replica_groups=mesh['groups'=2,'rows'=16] {'rows'}, dimensions={1}, use_global_device_ids=true | all-gather | bytes 278528 | tf_op jit(solution)/shard_map/all_gather | solution.py:67
  310.3 1.8 fusion.66
  312.2 2.9 cholesky.70
  315.8 0.7 fusion.41
  316.5 2.4 custom-call.14
  318.9 1.2 fusion.45
  320.2 0.7 copy-done.1
  321.6 23.4 %scatter_custom_fusion.2 = f32[32,2048]{0,1:T(8,128)} fusion(s32[4096]{0:T(1024)S(1)} %bitcast.100, f32[32,4096]{0,1:T(8,128)S(1)} %bitcast_multiply_fusion, f32[]{:T(128)} %constant.102.clone.1), kind=kCustom, calls=%fused_computation.12 | custom fusion | flops 131072 | bytes 2359300 | tf_op jit(solution)/shard_map/scatter-add | solution.py:77
  345.0 1.3 copy.57
  346.3 14.1 %gather_fusion.3 = f32[4096,32]{1,0:T(8,128)} fusion(f32[32,2048]{0,1:T(8,128)S(1)} %copy.57, s32[4096]{0:T(1024)S(1)} %bitcast_clamp_fusion), kind=kCustom, calls=%fused_computation.2.clone | custom fusion | bytes 1064960 | tf_op jit(solution)/shard_map/jit(_take)/gather | solution.py:73
  360.4 3.2 fusion.6
  363.6 36.6 %reduce-scatter.8.cloned.1.call-done = f32[32,128]{0,1:T(8,128)} async-done(((f32[32,2048]{0,1:T(8,128)}), f32[32,128]{0,1:T(8,128)}) %reduce-scatter.8.cloned.1.call-update) | async-done | bytes 16400 | tf_op jit(solution)/shard_map/reduce_scatter | solution.py:79
  400.2 1.2 fusion.39
  401.3 57.6 %psum.7 = f32[32,32]{0,1:T(8,128)S(1)} all-reduce(f32[32,32]{0,1:T(8,128)S(1)} %fusion.39), channel_id=1, replica_groups=mesh['groups'=2,'rows'=16] {'rows'}, use_global_device_ids=true, to_apply=%region_12.16 | all-reduce | flops 1024 | bytes 8192 | tf_op jit(solution)/shard_map/psum | solution.py:82
  459.0 2.9 cholesky.81
  462.0 0.6 compare_reduce_fusion
  462.6 0.7 fusion.42
  463.3 2.4 custom-call.9
  465.7 1.7 fusion.38
  (51 shorter events, 4.3 us)
Async XLA Ops:
  7.2 4.3 copy-start
  7.2 51.1 %all-gather.2.cloned.1.call-start = ((), (), s32[]{:S(2)}) async-start(), calls=%async_computation.3 | async-start | bytes 1114112 | tf_op jit(solution)/shard_map/all_gather | solution.py:44
  8.2 3.2 collective-permute-start
  11.5 3.7 copy-start.5
  11.5 3.9 copy-start.6
  15.1 158.6 %reduce-scatter.4.cloned.1.call-start = ((), (), s32[]{:S(2)}) async-start(), calls=%async_computation.4 | async-start | bytes 1114112 | tf_op jit(solution)/shard_map/reduce_scatter | solution.py:79
  41.0 17.3 %copy-start.4 = (bf16[128,256]{1,0:T(8,128)(2,1)S(1)}, bf16[128,256]{1,0:T(8,128)(2,1)}, u32[]{:S(2)}) copy-start(bf16[128,256]{1,0:T(8,128)(2,1)} %multiply_convert_fusion) | copy-start | bytes 196612
  93.0 267.4 %copy-start.3 = (f32[32,128]{1,0:T(8,128)}, f32[32,128]{1,0:T(8,128)S(1)}, u32[]{:S(2)}) copy-start(f32[32,128]{1,0:T(8,128)S(1)} %copy.61) | copy-start | bytes 49156
  117.0 169.9 %reduce-scatter.6.cloned.1.call-start = ((), (), s32[]{:S(2)}) async-start(), calls=%async_computation.5 | async-start | bytes 1114112 | tf_op jit(solution)/shard_map/reduce_scatter | solution.py:79
  206.9 0.7 copy-start.2
  231.8 168.4 %reduce-scatter.8.cloned.1.call-start = ((), (), s32[]{:S(2)}) async-start(), calls=%async_computation.6 | async-start | bytes 1114112 | tf_op jit(solution)/shard_map/reduce_scatter | solution.py:79
  320.2 0.7 copy-start.1
Sparse Core Ops, SparseCore 0:
  15.2 43.0 all-gather.1
  117.1 56.5 reduce-scatter.3
  231.9 54.9 reduce-scatter.5
  345.1 55.0 reduce-scatter.7
where the time goes:
time: 475 us; the launch traced here: 474 us
  waiting for transfers between devices  131 us (28%)
  blocking collectives  128 us (27%)
  other arithmetic  105 us (22%)
  local copies, waits for them, and re-layouts  81.2 us (17%)
  between operations  14 us (3%)
  matrix products  13.5 us (3%)
    reduce_scatter x3, waiting for transfers between devices, on_device(): lax.psum_scatter(spread, 'rows', scatter_dimension=1, tiled=True)  126 us
    all_gather x3, blocking collectives, on_device(): gathered = lax.all_gather(carried, 'rows', axis=1, tiled=True)  70.3 us
    scatter-add x3, other arithmetic, on_device(): spread = jnp.zeros((vec_count, gathered.shape[1]), jnp.float32).at[:, nei...  70.2 us
    psum x1, blocking collectives, on_device(): gram_matrix = lax.psum(partial_gram, 'rows')  57.6 us
    gather x3, local copies, waits for them, and re-layouts, on_device(): jnp.take(gathered, neighbours, axis=1)  42.3 us
    gather x3, local copies, waits for them, and re-layouts, one_block(): jnp.take_along_axis(scores, jnp.clip(relative, 0, block_cols - 1).T, axis=1)  32.9 us
    another operation x9, other arithmetic, on_device(): cholesky_factor = jnp.linalg.cholesky(gram_matrix)  10.8 us
    reduce_sum x3, other arithmetic, on_device(): jnp.sum(affinity[None] * jnp.take(gathered, neighbours, axis=1), axis=1)  9.57 us
  transfers between devices with their start and end apart: 5, of which 5 were waited for; matrix products, arithmetic and copies ran while one was open for 12% of the time, Pallas kernels for 0%

commit v1 on v0

--- a/solution.py
+++ b/solution.py
@@ -79,7 +79,7 @@
         mixed = 0.5 * (forward + lax.psum_scatter(spread, "rows", scatter_dimension=1, tiled=True))
         carried = mixed
     partial_gram = jnp.dot(carried, carried.T, precision=lax.Precision.HIGHEST)
-    gram_matrix = lax.psum(partial_gram, "rows")
+    gram_matrix = jnp.sum(lax.all_gather(partial_gram, "rows"), axis=0)
     cholesky_factor = jnp.linalg.cholesky(gram_matrix)
     carried = jax.scipy.linalg.solve_triangular(cholesky_factor, carried, lower=True)
     return (affinity, carried)

time: 475 us -> 437 us (0.920)
  blocking collectives: 128 us -> 90.4 us
    psum x1 -> x0, blocking collectives: 57.6 us -> none  [on_device(): gram_matrix = lax.psum(partial_gram, 'rows')]
    all_gather x0 -> x1, blocking collectives: none -> 20.1 us  [on_device(): gram_matrix = jnp.sum(lax.all_gather(partial_gram, 'rows'), axis=0)]
  transfers between devices with their start and end apart: 5 -> 5, of which waited for: 5 -> 5; matrix products, arithmetic and copies ran while one was open for 12% -> 13% of each run, Pallas kernels for 0% -> 0%
where the time goes in v1:
time: 437 us
  waiting for transfers between devices  131 us (30%)
  other arithmetic  105 us (24%)
  blocking collectives  90.4 us (21%)
  local copies, waits for them, and re-layouts  81.2 us (19%)
  between operations  14 us (3%)
  matrix products  13.5 us (3%)
    reduce_scatter x3, waiting for transfers between devices, on_device(): lax.psum_scatter(spread, 'rows', scatter_dimension=1, tiled=True)  126 us
    all_gather x3, blocking collectives, on_device(): gathered = lax.all_gather(carried, 'rows', axis=1, tiled=True)  70.3 us
    scatter-add x3, other arithmetic, on_device(): spread = jnp.zeros((vec_count, gathered.shape[1]), jnp.float32).at[:, nei...  70.2 us
    gather x3, local copies, waits for them, and re-layouts, on_device(): jnp.take(gathered, neighbours, axis=1)  42.3 us
    gather x3, local copies, waits for them, and re-layouts, one_block(): jnp.take_along_axis(scores, jnp.clip(relative, 0, block_cols - 1).T, axis=1)  32.9 us
    all_gather x1, blocking collectives, on_device(): gram_matrix = jnp.sum(lax.all_gather(partial_gram, 'rows'), axis=0)  20.1 us
    another operation x9, other arithmetic, on_device(): cholesky_factor = jnp.linalg.cholesky(gram_matrix)  10.8 us
    reduce_sum x3, other arithmetic, on_device(): jnp.sum(affinity[None] * jnp.take(gathered, neighbours, axis=1), axis=1)  9.57 us
  transfers between devices with their start and end apart: 5, of which 5 were waited for; matrix products, arithmetic and copies ran while one was open for 13% of the time, Pallas kernels for 0%

profile of v1, /device:TPU:0, one launch (start us, length us, event | category | flops | bytes accessed | tf_op | source)
XLA Modules:
  0.0 436.5 jit_solution(13941462872940119483)
XLA Ops:
  7.2 1.0 slice.17
  8.2 1.3 collective-permute-start
  9.5 0.7 broadcast_add_fusion
  10.2 1.3 collective-permute-done
  11.5 2.9 multiply_reduce_fusion
  14.3 0.7 multiply_convert_fusion
  15.4 25.2 %all_gather.19 = f32[32,2048]{1,0:T(8,128)S(1)} all-gather(f32[32,128]{1,0:T(8,128)S(1)} %convert_multiply_fusion), channel_id=1, replica_groups=mesh['groups'=2,'rows'=16] {'rows'}, dimensions={1}, use_global_device_ids=true | all-gather | bytes 278528 | tf_op jit(solution)/shard_map/all_gather | solution.py:67
  41.1 14.1 %gather_fusion.1 = f32[4096,32]{1,0:T(8,128)} fusion(f32[32,2048]{0,1:T(8,128)S(1)} %copy.61, s32[4096]{0:T(1024)S(1)} %bitcast_clamp_fusion), kind=kCustom, calls=%fused_computation.clone | custom fusion | bytes 1064960 | tf_op jit(solution)/shard_map/jit(_take)/gather | solution.py:73
  55.2 3.1 all-gather.3.cloned.1.call-done
  58.3 1.7 fusion.64
  60.0 32.8 %gather_fusion = f32[4096]{0:T(1024)S(1)} fusion(f32[128,2048]{1,0:T(8,128)S(1)} %fusion.64, s32[4096]{0:T(1024)S(1)} %reshape.113), kind=kCustom, calls=%fused_computation.3 | custom fusion | bytes 65536 | tf_op jit(solution)/shard_map/while/body/eval_jaxpr/jit(take_along_axis)/gather | solution.py:56
  93.6 23.4 %scatter_custom_fusion = f32[32,2048]{0,1:T(8,128)} fusion(s32[4096]{0:T(1024)S(1)} %bitcast.100, f32[32,4096]{0,1:T(8,128)S(1)} %bitcast_multiply_fusion.4, f32[]{:T(128)} %constant.102.clone.1), kind=kCustom, calls=%fused_computation.22 | custom fusion | flops 131072 | bytes 2359300 | tf_op jit(solution)/shard_map/scatter-add | solution.py:77
  117.1 3.2 fusion.12
  120.3 53.4 %reduce-scatter.4.cloned.1.call-done = f32[32,128]{0,1:T(8,128)} async-done(((f32[32,2048]{0,1:T(8,128)}), f32[32,128]{0,1:T(8,128)}) %reduce-scatter.4.cloned.1.call-update) | async-done | bytes 16400 | tf_op jit(solution)/shard_map/reduce_scatter | solution.py:79
  173.7 0.8 add_multiply_fusion.2
  174.6 22.6 %all_gather.20 = f32[32,2048]{0,1:T(8,128)S(1)} all-gather(f32[32,128]{0,1:T(8,128)S(1)} %add_multiply_fusion.2), channel_id=1, replica_groups=mesh['groups'=2,'rows'=16] {'rows'}, dimensions={1}, use_global_device_ids=true | all-gather | bytes 278528 | tf_op jit(solution)/shard_map/all_gather | solution.py:67
  197.1 1.8 fusion.65
  199.0 2.9 cholesky.59
  202.0 0.6 compare_reduce_fusion.2
  202.6 0.7 fusion.40
  203.3 2.4 custom-call.13
  205.7 1.2 fusion.48
  207.0 0.7 copy-done.1
  208.4 23.4 %scatter_custom_fusion.1 = f32[32,2048]{0,1:T(8,128)} fusion(s32[4096]{0:T(1024)S(1)} %bitcast.101, f32[32,4096]{0,1:T(8,128)S(1)} %bitcast_multiply_fusion.2, f32[]{:T(128)} %constant.102.clone.1), kind=kCustom, calls=%fused_computation.17 | custom fusion | flops 131072 | bytes 2359300 | tf_op jit(solution)/shard_map/scatter-add | solution.py:77
  232.0 1.3 copy.65
  233.3 14.1 %gather_fusion.2 = f32[4096,32]{1,0:T(8,128)} fusion(f32[32,2048]{0,1:T(8,128)S(1)} %copy.65, s32[4096]{0:T(1024)S(1)} %bitcast_clamp_fusion), kind=kCustom, calls=%fused_computation.1.clone | custom fusion | bytes 1064960 | tf_op jit(solution)/shard_map/jit(_take)/gather | solution.py:73
  247.4 3.2 fusion.9
  250.6 36.3 %reduce-scatter.6.cloned.1.call-done = f32[32,128]{0,1:T(8,128)} async-done(((f32[32,2048]{0,1:T(8,128)}), f32[32,128]{0,1:T(8,128)}) %reduce-scatter.6.cloned.1.call-update) | async-done | bytes 16400 | tf_op jit(solution)/shard_map/reduce_scatter | solution.py:79
  286.9 0.8 add_multiply_fusion.1
  287.8 22.6 %all_gather.21 = f32[32,2048]{0,1:T(8,128)S(1)} all-gather(f32[32,128]{0,1:T(8,128)S(1)} %add_multiply_fusion.1), channel_id=1, replica_groups=mesh['groups'=2,'rows'=16] {'rows'}, dimensions={1}, use_global_device_ids=true | all-gather | bytes 278528 | tf_op jit(solution)/shard_map/all_gather | solution.py:67
  310.3 1.8 fusion.66
  312.2 2.9 cholesky.70
  315.2 0.6 compare_reduce_fusion.1
  315.8 0.7 fusion.41
  316.5 2.4 custom-call.14
  318.9 1.2 fusion.45
  320.2 0.7 copy-done.2
  321.6 23.4 %scatter_custom_fusion.2 = f32[32,2048]{0,1:T(8,128)} fusion(s32[4096]{0:T(1024)S(1)} %bitcast.102, f32[32,4096]{0,1:T(8,128)S(1)} %bitcast_multiply_fusion, f32[]{:T(128)} %constant.102.clone.1), kind=kCustom, calls=%fused_computation.12 | custom fusion | flops 131072 | bytes 2359300 | tf_op jit(solution)/shard_map/scatter-add | solution.py:77
  345.0 1.3 copy.68
  346.3 14.1 %gather_fusion.3 = f32[4096,32]{1,0:T(8,128)} fusion(f32[32,2048]{0,1:T(8,128)S(1)} %copy.68, s32[4096]{0:T(1024)S(1)} %bitcast_clamp_fusion), kind=kCustom, calls=%fused_computation.2.clone | custom fusion | bytes 1064960 | tf_op jit(solution)/shard_map/jit(_take)/gather | solution.py:73
  360.4 3.2 fusion.6
  363.6 36.6 %reduce-scatter.8.cloned.1.call-done = f32[32,128]{0,1:T(8,128)} async-done(((f32[32,2048]{0,1:T(8,128)}), f32[32,128]{0,1:T(8,128)}) %reduce-scatter.8.cloned.1.call-update) | async-done | bytes 16400 | tf_op jit(solution)/shard_map/reduce_scatter | solution.py:79
  400.2 1.2 fusion.39
  401.3 20.1 %all-gather = f32[512,32]{1,0:T(8,128)S(1)} all-gather(f32[32,32]{1,0:T(8,128)S(1)} %fusion.39), channel_id=2, replica_groups=mesh['groups'=2,'rows'=16] {'rows'}, dimensions={0}, use_global_device_ids=true | all-gather | bytes 69632 | tf_op jit(solution)/shard_map/all_gather | solution.py:82
  421.6 2.9 cholesky.81
  425.2 0.7 fusion.42
  425.8 2.4 custom-call.9
  428.3 1.7 fusion.38
  (52 shorter events, 4.4 us)
Async XLA Ops:
  7.2 4.3 copy-start
  7.2 51.1 %all-gather.3.cloned.1.call-start = ((), (), s32[]{:S(2)}) async-start(), calls=%async_computation.3 | async-start | bytes 1114112 | tf_op jit(solution)/shard_map/all_gather | solution.py:44
  8.2 3.2 collective-permute-start
  11.5 3.7 copy-start.5
  11.5 3.9 copy-start.6
  15.1 158.6 %reduce-scatter.4.cloned.1.call-start = ((), (), s32[]{:S(2)}) async-start(), calls=%async_computation.4 | async-start | bytes 1114112 | tf_op jit(solution)/shard_map/reduce_scatter | solution.py:79
  41.0 17.3 %copy-start.4 = (bf16[128,256]{1,0:T(8,128)(2,1)S(1)}, bf16[128,256]{1,0:T(8,128)(2,1)}, u32[]{:S(2)}) copy-start(bf16[128,256]{1,0:T(8,128)(2,1)} %multiply_convert_fusion) | copy-start | bytes 196612
  93.0 267.4 %copy-start.3 = (f32[32,128]{1,0:T(8,128)}, f32[32,128]{1,0:T(8,128)S(1)}, u32[]{:S(2)}) copy-start(f32[32,128]{1,0:T(8,128)S(1)} %copy.71) | copy-start | bytes 49156
  117.0 169.9 %reduce-scatter.6.cloned.1.call-start = ((), (), s32[]{:S(2)}) async-start(), calls=%async_computation.5 | async-start | bytes 1114112 | tf_op jit(solution)/shard_map/reduce_scatter | solution.py:79
  206.9 0.7 copy-start.1
  231.8 168.4 %reduce-scatter.8.cloned.1.call-start = ((), (), s32[]{:S(2)}) async-start(), calls=%async_computation.6 | async-start | bytes 1114112 | tf_op jit(solution)/shard_map/reduce_scatter | solution.py:79
  320.2 0.7 copy-start.2
Sparse Core Ops, SparseCore 0:
  15.2 43.0 all-gather.2
  117.1 56.5 reduce-scatter.3
  231.9 54.9 reduce-scatter.5
  345.1 55.0 reduce-scatter.7
